TPU v7x, 128 devices: a whole 4x4x4 slice. The times are simulated.
128 devices in a mesh: dp: 8 (over y, core), expert: 16 (over z, x).
Axes of the slice: x: 4, y: 4, z: 4, core: 2. Of those that a mesh axis runs over, the one named last changes fastest.
Arguments:
- tokens: bfloat16 [8, 4, 8192, 1024], P('dp', None, 'expert'), may hold values from -8000 to 8000
- slot_params: bfloat16 [1024, 256], replicated, may hold values from -8 to 8
- dest: int32 [8, 4, 32], P('dp', None, 'expert'), may hold values from 0 to 127, as said below
- lengths: int32 [8, 4], P('dp'), may hold values from 256 to 8192
- w_in: bfloat16 [128, 1024, 4096], P('expert', None, 'dp'), may hold values from -0.1875 to 0.1875
- w_out: bfloat16 [128, 4096, 1024], P('expert', 'dp'), may hold values from -3 to 3
Outputs:
- mixed: bfloat16 [8, 128, 256, 1024], P('dp', 'expert')
Inputs may be any that keep to these rules, and one draw needn't show every extreme that they name: For each g, dest[g] holds every number of 0 to 127 once; the 8 blocks held by one device (block indices j from k * 2 on, for every q) go to output blocks of different devices, device d holding output blocks d * 4 * 2 onward, so each device receives at most one block from each device.
All inputs are finite; a program needn't handle non-finite values.
Results may differ from a plain program's by a relative error of at most 0.01.
Values may be sent and summed in bfloat16 or wider, within the bound.
No kernel may reach another device: no remote copies, remote signals or barrier semaphores. Data moves between devices by JAX's collectives and lax.ppermute only.
A program may use at most 128 MiB of HBM per device.

v0:
```python
import math

import jax
import jax.numpy as jnp
from jax import lax
from jax.sharding import Mesh
from jax.sharding import PartitionSpec as P

EXPERT = ("expert_0", "expert_1")


def over_axes(array, axes):
    for axis in axes:
        array = lax.pmax(array, axis)
    return array


def in_blocks(array, dim, peers):
    before, after = (array.shape[:dim], array.shape[dim + 1 :])
    return jnp.moveaxis(array.reshape(*before, peers, -1, *after), dim, 0)


def summed_on_arrival(array, axis, dim):
    peers = lax.axis_size(axis)
    tiles = lax.all_to_all(in_blocks(array, dim, peers), axis, 0, 0, tiled=True)
    return jnp.sum(tiles.astype(jnp.float32), axis=0)


def in_one_piece(arrays, axis, dim, along):
    widths = [math.prod(a.shape[along:]) for a in arrays]
    both = jnp.concatenate(
        [a.reshape(*a.shape[:along], w) for a, w in zip(arrays, widths)], axis=along
    )
    filled = summed_on_arrival(both, axis, dim)
    tiles = jnp.split(filled, [sum(widths[:k]) for k in range(1, len(widths))], axis=along)
    return tuple(
        (b.reshape(*filled.shape[:along], *a.shape[along:]) for a, b in zip(arrays, tiles))
    )


def in_order(tiles, dim):
    tiles = jnp.moveaxis(tiles, 0, dim)
    dims = tiles.shape
    return tiles.reshape(*dims[:dim], dims[dim] * dims[dim + 1], *dims[dim + 2 :])


def copy_for_each(array, axis):
    copies = jnp.broadcast_to(array, (lax.axis_size(axis), *array.shape))
    return lax.all_to_all(copies, axis, split_axis=0, concat_axis=0, tiled=True)


def gathered_copies(array, axis, dim):
    return in_order(copy_for_each(array, axis), dim)


def sum_at_owner(array, axis, dim):
    tiles = in_blocks(array, dim, lax.axis_size(axis))
    arrived = lax.all_to_all(tiles, axis, split_axis=0, concat_axis=0, tiled=True)
    return arrived.sum(axis=0)


def arrange(labels, wanted):
    matches = labels[None, :] == jnp.arange(wanted, dtype=jnp.int32)[:, None]
    senders = jnp.arange(labels.shape[0], dtype=jnp.int32)[None, :]
    return jnp.sum(jnp.where(matches, senders, 0), axis=1)


def local(tokens, slot_params, dest, lengths, w_in, w_out):
    seq_count = tokens.shape[1]
    blocks_here = dest.shape[2]
    width = tokens.shape[3]
    block_tokens = tokens.shape[2] // blocks_here
    held_blocks = seq_count * blocks_here
    shard_count = lax.axis_size(EXPERT)
    shard_index = lax.axis_index(EXPERT)
    block_total = blocks_here * shard_count
    slots_total = slot_params.shape[1]
    owned_slots = slots_total // shard_count
    block_local = tokens.reshape(held_blocks, block_tokens, width)
    targets = dest.reshape(held_blocks)
    ordinal = jnp.arange(held_blocks, dtype=jnp.int32)
    source_ids = (
        ordinal // blocks_here * block_total + shard_index * blocks_here + ordinal % blocks_here
    )
    peer_device = targets // held_blocks
    dest_slot = targets % held_blocks
    seq_lengths = lengths[0]
    seq_of = source_ids // block_total
    place_of = source_ids % block_total
    member = seq_of[:, None] == jnp.arange(seq_count, dtype=jnp.int32)[None, :]
    length_of = jnp.sum(jnp.where(member, seq_lengths[None, :], 0), axis=1)
    token_place = (
        place_of[:, None] * block_tokens + jnp.arange(block_tokens, dtype=jnp.int32)[None, :]
    )
    live_mask = token_place < length_of[:, None]
    logits = jnp.dot(
        block_local.reshape(held_blocks * block_tokens, width),
        slot_params,
        preferred_element_type=jnp.float32,
    )
    logits = logits.reshape(held_blocks, block_tokens, slots_total)
    masked = jnp.where(live_mask[..., None], logits, -jnp.inf)
    block_top = jnp.max(masked, axis=1)
    seq_top = jnp.max(jnp.where(member[:, :, None], block_top[:, None, :], -jnp.inf), axis=0)
    top = over_axes(seq_top, EXPERT)
    block_ref = jnp.sum(jnp.where(member[:, :, None], top[None, :, :], 0.0), axis=1)
    weight = jnp.where(live_mask[..., None], jnp.exp(logits - block_ref[:, None, :]), 0.0)
    block_mass = jnp.sum(weight, axis=1)
    seq_mass = jnp.sum(jnp.where(member[:, :, None], block_mass[:, None, :], 0.0), axis=0)
    block_numer = jnp.einsum(
        "bts,btd->bsd", weight.astype(jnp.bfloat16), block_local, preferred_element_type=jnp.float32
    )
    seq_numer = jnp.einsum(
        "bq,bsd->qsd", member.astype(jnp.float32), block_numer, precision=lax.Precision.HIGHEST
    )
    numer_own, mass_own = in_one_piece(
        (seq_numer.astype(jnp.bfloat16), seq_mass.astype(jnp.bfloat16)), EXPERT, 1, 2
    )
    slot_in = (numer_own / mass_own[..., None]).astype(jnp.bfloat16)
    gathered = gathered_copies(slot_in, "dp", 0)
    experts_here = w_in.shape[0]
    per_expert = owned_slots // experts_here
    grouped = gathered.reshape(gathered.shape[0], experts_here, per_expert, width)
    hidden = jax.nn.gelu(
        jnp.einsum("nepd,edh->neph", grouped, w_in, preferred_element_type=jnp.float32)
    ).astype(jnp.bfloat16)
    result = jnp.einsum("neph,ehd->nepd", hidden, w_out, preferred_element_type=jnp.float32)
    slot_out = sum_at_owner(
        result.reshape(seq_count * lax.axis_size("dp"), owned_slots, width), "dp", 0
    ).astype(jnp.bfloat16)
    mix = jax.nn.softmax(logits, axis=-1).astype(jnp.bfloat16)
    chosen = gathered_copies(slot_out, EXPERT, 1)[seq_of]
    combined = jnp.einsum("bts,bsd->btd", mix, chosen, preferred_element_type=jnp.float32)
    finished = jnp.where(live_mask[..., None], combined, 0.0).astype(jnp.bfloat16)
    outgoing = (
        jnp.zeros((shard_count, block_tokens, width), jnp.bfloat16).at[peer_device].set(finished)
    )
    labels = jnp.full((shard_count,), -1, jnp.int32).at[peer_device].set(dest_slot)
    arrived, arrived_labels = (
        lax.all_to_all(outgoing, EXPERT, split_axis=0, concat_axis=0, tiled=True),
        lax.all_to_all(labels, EXPERT, split_axis=0, concat_axis=0, tiled=True),
    )
    result = arrived[arrange(arrived_labels, held_blocks)]
    return result.reshape(1, held_blocks, block_tokens, width)


def solution(mesh):
    finer = Mesh(mesh.devices.reshape(mesh.shape["dp"], 4, 4), ("dp", "expert_0", "expert_1"))
    in_specs = (
        P("dp", None, EXPERT, None),
        P(),
        P("dp", None, EXPERT),
        P("dp", None),
        P(EXPERT, None, "dp"),
        P(EXPERT, "dp", None),
    )
    out_specs = P("dp", EXPERT, None, None)
    return jax.shard_map(local, mesh=finer, in_specs=in_specs, out_specs=out_specs, check_vma=False)
```

profile of v0, /device:TPU:0, one launch (start us, length us, event | category | flops | bytes accessed | tf_op | source)
XLA Modules:
  0.0 359.7 jit_solution(15317321631141466556)
XLA Ops:
  0.0 0.8 select_reduce_fusion.5
  0.9 0.2 copy-done
  1.1 3.2 select_reduce_fusion
  4.3 0.1 select_reduce_fusion.3
  4.4 11.9 %pmax.14 = f32[4,256]{1,0:T(4,128)S(1)} all-reduce(f32[4,256]{1,0:T(4,128)S(1)} %select_reduce_fusion.3), channel_id=1, replica_groups=mesh['dp'=8,'expert_0'=4,'expert_1'=4] {'expert_0'}, use_global_device_ids=true, to_apply=%region_5.6 | all-reduce | flops 1024 | bytes 8192 | tf_op jit(solution)/shard_map/pmax | solution.py:14
  16.3 10.5 %pmax.15 = f32[4,256]{1,0:T(4,128)S(1)} all-reduce(f32[4,256]{1,0:T(4,128)S(1)} %pmax.14), channel_id=1, replica_groups=mesh['dp'=8,'expert_0'=4,'expert_1'=4] {'expert_1'}, use_global_device_ids=true, to_apply=%region_6.7 | all-reduce | flops 1024 | bytes 8192 | tf_op jit(solution)/shard_map/pmax | solution.py:14
  26.7 0.1 select_reduce_fusion.2
  26.8 0.5 fusion.10
  27.3 6.8 %fusion.30 = f32[8,256,1024]{2,1,0:T(8,128)} fusion(bf16[8,256,1024]{2,1,0:T(8,128)(2,1)} %bitcast.72, f32[8,256,256]{2,1,0:T(8,128)S(1)} %get-tuple-element.6, f32[8,256]{1,0:T(8,128)S(1)} %select_reduce_fusion.2, pred[8,256]{1,0:T(8,128)(4,1)S(1)} %add_compare_fusion), kind=kOutput, calls=%fused_computation.32 | convolution fusion | flops 1075314688 | bytes 14690304 | tf_op jit(solution)/shard_map/bts,btd->bsd/dot_general | solution.py:110
  34.1 0.1 select_reduce_fusion.1
  34.2 0.1 convert_element_type.43
  34.3 0.5 copy.47
  34.8 12.1 %fusion.7 = bf16[4,256,1024]{2,0,1:T(4,128)(2,1)S(1)} fusion(f32[8,256,1024]{2,1,0:T(8,128)} %fusion.30, s32[8]{0:T(128)S(1)} %get-tuple-element.7), kind=kOutput, calls=%fused_computation.18 | convolution fusion | flops 101711904 | bytes 10485792 | tf_op jit(solution)/shard_map/bq,bsd->qsd/dot_general | solution.py:113
  46.8 1.4 maximum_bitcast_fusion
  48.2 30.7 %all_to_all.34 = bf16[16,4,16,1025]{3,1,2,0:T(4,128)(2,1)S(1)} all-to-all(bf16[16,4,16,1025]{3,1,2,0:T(4,128)(2,1)S(1)} %maximum_bitcast_fusion), channel_id=1, replica_groups=mesh['dp'=8,'expert_0'=4,'expert_1'=4] {'expert_0','expert_1'}, dimensions={0} | all-to-all | bytes 4198400 | tf_op jit(solution)/shard_map/all_to_all | solution.py:25
  78.9 1.0 convert_reduce_fusion
  80.0 0.1 copy.48
  80.1 0.1 copy.49
  80.2 0.1 fusion.44
  80.3 0.4 broadcast_in_dim.150
  80.7 20.2 %all_to_all.35 = bf16[8,4,16,1024]{3,1,2,0:T(4,128)(2,1)S(1)} all-to-all(bf16[8,4,16,1024]{3,1,2,0:T(4,128)(2,1)S(1)} %broadcast_in_dim.150), channel_id=1, replica_groups=mesh['dp'=8,'expert_0'=4,'expert_1'=4] {'dp'}, dimensions={0} | all-to-all | bytes 2097152 | tf_op jit(solution)/shard_map/all_to_all | solution.py:49
  100.9 1.5 copy.50
  102.4 2.2 reshape_reshape.7
  104.5 10.4 %fusion.12 = f32[32,8,2,1024]{3,0,2,1:T(8,128)} fusion(bf16[8,512,1024]{2,1,0:T(8,128)(2,1)} %param.11, bf16[32,8,2,1024]{3,0,2,1:T(8,128)(2,1)} %reshape_reshape.7, bf16[8,1024,512]{2,1,0:T(8,128)(2,1)} %param.10), kind=kOutput, calls=%fused_computation.21 | convolution fusion | flops 1076101120 | bytes 19922944 | tf_op jit(solution)/shard_map/neph,ehd->nepd/dot_general | solution.py:127
  114.9 2.9 reshape_reshape.8
  117.8 1.8 copy.51
  119.6 30.4 %all_to_all.36 = f32[8,4,16,1024]{3,1,2,0:T(4,128)} all-to-all(f32[8,4,16,1024]{3,1,2,0:T(4,128)S(1)} %copy.51), channel_id=1, replica_groups=mesh['dp'=8,'expert_0'=4,'expert_1'=4] {'dp'}, dimensions={0} | all-to-all | bytes 4194304 | tf_op jit(solution)/shard_map/all_to_all | solution.py:58
  149.9 2.2 reduce_sum.80
  152.2 1.6 broadcast_in_dim.151
  153.7 4.4 %all-to-all-start.3 = ((bf16[16,4,16,1024]{3,2,1,0:T(8,128)(2,1)}), bf16[16,4,16,1024]{3,2,1,0:T(8,128)(2,1)}, u32[]{:S(2)}, u32[]{:S(2)}) async-start(bf16[16,4,16,1024]{3,2,1,0:T(8,128)(2,1)} %broadcast_in_dim.151), calls=%async_computation.3 | async-start | bytes 4194304 | tf_op jit(solution)/shard_map/all_to_all | solution.py:49
  158.2 0.1 copy.44
  158.3 0.1 reshape.318
  158.4 0.1 reshape.320
  158.5 0.6 scatter_custom_fusion.1
  159.1 0.7 copy.56
  159.8 0.6 fusion.65
  160.4 29.3 %all-to-all-done.3 = bf16[16,4,16,1024]{3,2,1,0:T(8,128)(2,1)} async-done(((bf16[16,4,16,1024]{3,2,1,0:T(8,128)(2,1)}), bf16[16,4,16,1024]{3,2,1,0:T(8,128)(2,1)}, u32[]{:S(2)}, u32[]{:S(2)}) %all-to-all-start.3) | async-done | bytes 2097184 | tf_op jit(solution)/shard_map/all_to_all | solution.py:49
  189.7 3.5 all-to-all-start.5
  193.2 3.2 copy.54
  196.4 4.4 %gather_fusion = bf16[8,256,1024]{2,1,0:T(8,128)(2,1)} fusion(bf16[4,256,1024]{2,1,0:T(8,128)(2,1)} %bitcast.69, s32[1024]{0:T(1024)S(1)} %pad_clamp_fusion.1), kind=kCustom, calls=%fused_computation | custom fusion | bytes 8388640 | tf_op jit(solution)/shard_map/gather | solution.py:132
  200.9 7.9 %select_convert_fusion = bf16[8,256,1024]{2,1,0:T(8,128)(2,1)} fusion(pred[8,256]{1,0:T(8,128)(4,1)S(1)} %add_compare_fusion, bf16[8,256,1024]{2,1,0:T(8,128)(2,1)} %gather_fusion, f32[8,256]{1,0:T(8,128)S(1)} %fusion.65, f32[8,256,256]{2,1,0:T(8,128)S(1)} %get-tuple-element.6), kind=kOutput, calls=%fused_computation.11 | convolution fusion | flops 1079511296 | bytes 10496000 | tf_op jit(solution)/shard_map/bts,bsd->btd/dot_general | solution.py:133
  208.8 4.3 %broadcast_in_dim.136 = bf16[16,256,1024]{2,1,0:T(8,128)(2,1)} broadcast(bf16[]{:T(256)} %constant.84.clone.1), dimensions={} | broadcast | bytes 8388610 | tf_op jit(solution)/shard_map/broadcast_in_dim | solution.py:136
  213.1 10.9 %scatter_fusion = bf16[16,256,1024]{2,1,0:T(8,128)(2,1)} fusion(bf16[16,256,1024]{2,1,0:T(8,128)(2,1)} %broadcast_in_dim.136, s32[8]{0:T(128)S(1)} %fusion.54, bf16[8,256,1024]{2,1,0:T(8,128)(2,1)} %select_convert_fusion), kind=kCustom, calls=%fused_computation.2 | custom fusion | bytes 12582944 | tf_op jit(solution)/shard_map/scatter | solution.py:136
  224.0 7.4 %all-to-all-start.4 = ((bf16[16,256,1024]{2,1,0:T(8,128)(2,1)}), bf16[16,256,1024]{2,1,0:T(8,128)(2,1)}, u32[]{:S(2)}, u32[]{:S(2)}) async-start(bf16[16,256,1024]{2,1,0:T(8,128)(2,1)} %scatter_fusion), calls=%async_computation.4 | async-start | bytes 16777216 | tf_op jit(solution)/shard_map/all_to_all | solution.py:140
  231.4 0.4 reduce
  231.7 0.1 select_reduce_fusion.4
  231.9 121.6 %all-to-all-done.4 = bf16[16,256,1024]{2,1,0:T(8,128)(2,1)} async-done(((bf16[16,256,1024]{2,1,0:T(8,128)(2,1)}), bf16[16,256,1024]{2,1,0:T(8,128)(2,1)}, u32[]{:S(2)}, u32[]{:S(2)}) %all-to-all-start.4) | async-done | bytes 8388640 | tf_op jit(solution)/shard_map/all_to_all | solution.py:140
  353.5 6.2 %gather_fusion.1 = bf16[8,256,1024]{2,1,0:T(8,128)(2,1)} fusion(bf16[16,256,1024]{2,1,0:T(8,128)(2,1)} %all-to-all-done.4, s32[1024]{0:T(1024)S(1)} %pad_clamp_fusion), kind=kCustom, calls=%fused_computation.1 | custom fusion | bytes 8388640 | tf_op jit(solution)/shard_map/gather | solution.py:143
  (17 shorter events, 0.2 us)
Async XLA Ops:
  0.0 1.1 copy-start
  149.9 8.3 %copy-start.2 = (s32[1,4,2]{1,2,0:T(2,128)S(1)}, s32[1,4,2]{1,2,0:T(2,128)}, u32[]{:S(2)}) copy-start(s32[1,4,2]{1,2,0:T(2,128)} %param.8) | copy-start | bytes 100
  153.7 36.0 %all-to-all-start.3 = ((bf16[16,4,16,1024]{3,2,1,0:T(8,128)(2,1)}), bf16[16,4,16,1024]{3,2,1,0:T(8,128)(2,1)}, u32[]{:S(2)}, u32[]{:S(2)}) async-start(bf16[16,4,16,1024]{3,2,1,0:T(8,128)(2,1)} %broadcast_in_dim.151), calls=%async_computation.3 | async-start | bytes 4194304 | tf_op jit(solution)/shard_map/all_to_all | solution.py:49
  189.7 34.3 %all-to-all-start.5 = ((s32[16,1,1]{2,1,0:T(1,128)}), s32[16,1,1]{2,1,0:T(1,128)S(1)}, u32[]{:S(2)}, u32[]{:S(2)}) async-start(s32[16,1,1]{2,1,0:T(1,128)} %copy.56), calls=%async_computation.5 | async-start | bytes 16384 | tf_op jit(solution)/shard_map/all_to_all | solution.py:141
  224.0 129.5 %all-to-all-start.4 = ((bf16[16,256,1024]{2,1,0:T(8,128)(2,1)}), bf16[16,256,1024]{2,1,0:T(8,128)(2,1)}, u32[]{:S(2)}, u32[]{:S(2)}) async-start(bf16[16,256,1024]{2,1,0:T(8,128)(2,1)} %scatter_fusion), calls=%async_computation.4 | async-start | bytes 16777216 | tf_op jit(solution)/shard_map/all_to_all | solution.py:140
  231.9 127.8 %copy-start.1 = (bf16[1024,256]{1,0:T(8,128)(2,1)S(1)}, bf16[1024,256]{1,0:T(8,128)(2,1)}, u32[]{:S(2)}) copy-start(bf16[1024,256]{1,0:T(8,128)(2,1)} %param.7) | copy-start | bytes 1572868
where the time goes:
time: 361 us; the launch traced here: 360 us
  waiting for transfers between devices  151 us (42%)
  blocking collectives  104 us (29%)
  local copies, waits for them, and re-layouts  41.7 us (12%)
  matrix products  40.4 us (11%)
  starting transfers between devices  15.3 us (4%)
  other arithmetic  7.51 us (2%)
    all_to_all x1, waiting for transfers between devices, local(): lax.all_to_all(outgoing, EXPERT, split_axis=0, concat_axis=0, tiled=True)  122 us
    all_to_all x1, blocking collectives, summed_on_arrival(): tiles = lax.all_to_all(in_blocks(array, dim, peers), axis, 0, 0, tiled=True)  30.7 us
    all_to_all x1, blocking collectives, sum_at_owner(): lax.all_to_all(tiles, axis, split_axis=0, concat_axis=0, tiled=True)  30.4 us
    all_to_all x1, waiting for transfers between devices, copy_for_each(): return lax.all_to_all(copies, axis, split_axis=0, concat_axis=0, tiled=True)  29.3 us
    pmax x2, blocking collectives, over_axes(): array = lax.pmax(array, axis)  22.4 us
    all_to_all x1, blocking collectives, copy_for_each(): return lax.all_to_all(copies, axis, split_axis=0, concat_axis=0, tiled=True)  20.2 us
    dot_general x1, matrix products, local(): jnp.einsum('bq,bsd->qsd', member.astype(jnp.float32), block_numer, precis...  12.1 us
    scatter x1, local copies, waits for them, and re-layouts, local(): jnp.zeros((shard_count, block_tokens, width), jnp.bfloat16).at[peer_device]  10.9 us
  transfers between devices with their start and end apart: 3, of which 2 were waited for; matrix products, arithmetic and copies ran while one was open for 9% of the time, Pallas kernels for 0%

commit v1 on v0

v1 whole, which is shorter than its diff:
```python
import functools
import math

import jax
import jax.numpy as jnp
from jax import lax
from jax.experimental import pallas as pl
from jax.experimental.pallas import tpu as pltpu
from jax.sharding import Mesh
from jax.sharding import PartitionSpec as P

DP = ("y", "c")
EXPERT = ("z", "x")
LANES = 128
PIECES = 8
NO_TOKEN = -1e30
F32 = jnp.float32
BF16 = jnp.bfloat16


def pieces_of(value):
    high = value.astype(BF16).astype(F32)
    rest = value - high
    middle = rest.astype(BF16).astype(F32)
    return high, middle, rest - middle


def dispatch_kernel(counts, peers, labels, tokens, params, payload, mixes, stats):
    q = pl.program_id(0)
    last = pl.num_programs(0) - 1
    feats = tokens[0, 0]
    length = feats.shape[0]
    shards = payload.shape[0]
    slots = params.shape[1]
    owned = slots // shards
    slabs = feats.shape[1] // LANES
    stat_rows = payload.shape[1] - owned
    seqs = stat_rows // (slabs * owned)
    block = mixes.shape[1]

    @pl.when(q == 0)
    def _():
        mixes[...] = jnp.zeros(mixes.shape, mixes.dtype)
        stats[...] = jnp.zeros(stats.shape, stats.dtype)

    logits = jnp.dot(feats, params[...], preferred_element_type=F32)
    live = lax.broadcasted_iota(jnp.int32, (length, 1), 0) < counts[q]
    masked = jnp.where(live, logits, NO_TOKEN)
    top = jnp.max(masked, axis=0, keepdims=True)
    weight = jnp.where(live, jnp.exp(masked - top), 0.0)
    mass = jnp.sum(weight, axis=0, keepdims=True)
    numer = lax.dot_general(
        weight.astype(BF16), feats, (((0,), (0,)), ((), ())), preferred_element_type=F32
    ).astype(BF16)
    for j in range(slabs):
        start = pl.multiple_of(j * seqs * owned + q * owned, owned)
        piece = numer[:, j * LANES : (j + 1) * LANES]
        payload[:, pl.ds(start, owned), :] = piece.reshape(shards, owned, LANES)

    row = lax.broadcasted_iota(jnp.int32, (PIECES, slots), 0)
    stacked = jnp.zeros((PIECES, slots), F32)
    for k, part in enumerate(pieces_of(top) + pieces_of(mass)):
        stacked = jnp.where(row == k, part, stacked)
    stats[pl.ds(pl.multiple_of(q * PIECES, PIECES), PIECES), :] = stacked

    peak = jnp.max(logits, axis=1, keepdims=True)
    raised = jnp.exp(logits - peak)
    mix = raised / jnp.sum(raised, axis=1, keepdims=True)
    mix = jnp.where(live, mix, 0.0).astype(BF16)
    per_seq = length // block
    for j in range(per_seq):
        mixes[peers[q * per_seq + j]] = mix[j * block : (j + 1) * block]

    @pl.when(q == last)
    def _():
        turned = stats[...].T
        lane = lax.broadcasted_iota(jnp.int32, (owned, LANES), 1)
        for d in range(shards):
            mine = turned[d * owned : (d + 1) * owned]
            mine = jnp.where(lane == LANES - 1, labels[d].astype(F32), mine)
            payload[d, stat_rows:, :] = mine.astype(BF16)


def dispatch(tokens, params, counts, peers, labels, shards):
    seqs, length, width = tokens.shape[1:]
    slots = params.shape[1]
    owned = slots // shards
    rows = width // LANES * seqs * owned + owned
    block = length * seqs // peers.shape[0]
    return pl.pallas_call(
        dispatch_kernel,
        grid_spec=pltpu.PrefetchScalarGridSpec(
            num_scalar_prefetch=3,
            grid=(seqs,),
            in_specs=[
                pl.BlockSpec((1, 1, length, width), lambda q, *_: (0, q, 0, 0)),
                pl.BlockSpec((width, slots), lambda q, *_: (0, 0)),
            ],
            out_specs=[
                pl.BlockSpec((shards, rows, LANES), lambda q, *_: (0, 0, 0)),
                pl.BlockSpec((shards, block, slots), lambda q, *_: (0, 0, 0)),
            ],
            scratch_shapes=[pltpu.VMEM((LANES, slots), F32)],
        ),
        out_shape=[
            jax.ShapeDtypeStruct((shards, rows, LANES), BF16),
            jax.ShapeDtypeStruct((shards, block, slots), BF16),
        ],
        name="dispatch",
    )(counts, peers, labels, tokens, params)


def expert_order(seqs, experts, per_expert, back):
    total = seqs * experts * per_expert
    here = lax.broadcasted_iota(jnp.int32, (total, total), 1 if back else 0)
    there = lax.broadcasted_iota(jnp.int32, (total, total), 0 if back else 1)
    expert = here // (seqs * per_expert)
    seq = here // per_expert % seqs
    rank = here % per_expert
    return (there == (seq * experts + expert) * per_expert + rank).astype(BF16)


def own_kernel(seqs, experts, received, result, labels):
    shards, rows, _ = received.shape
    owned = result.shape[1] // seqs
    stat_rows = rows - owned
    slabs = stat_rows // (seqs * owned)
    raw = received[:, stat_rows:, :].astype(F32)
    labels[...] = raw[:, 0, :]
    joined = raw + pltpu.roll(raw, LANES - 1, 2) + pltpu.roll(raw, LANES - 2, 2)
    top = jnp.max(joined, axis=0, keepdims=True)
    factor = jnp.exp(joined - top)
    mass = jnp.sum(joined * pltpu.roll(factor, 3, 2), axis=0, keepdims=True)
    scale = factor / pltpu.roll(mass, LANES - 3, 2)
    parts = []
    for q in range(seqs):
        totals = [jnp.zeros((owned, LANES), F32)] * slabs
        for s in range(shards):
            column = scale[s, :, q * PIECES : q * PIECES + 1]
            for j in range(slabs):
                start = (j * seqs + q) * owned
                totals[j] += received[s, start : start + owned, :].astype(F32) * column
        parts.append(jnp.concatenate(totals, axis=1))
    slot_in = jnp.concatenate(parts, axis=0).astype(BF16)
    order = expert_order(seqs, experts, owned // experts, False)
    ordered = jnp.dot(order, slot_in, preferred_element_type=F32).astype(BF16)
    for y in range(result.shape[0]):
        result[y] = ordered


def own_slots(received, seqs, experts, copies, owned):
    shards, rows, _ = received.shape
    width = (rows - owned) // (seqs * owned) * LANES
    return pl.pallas_call(
        functools.partial(own_kernel, seqs, experts),
        out_shape=[
            jax.ShapeDtypeStruct((copies, seqs * owned, width), BF16),
            jax.ShapeDtypeStruct((shards, LANES), F32),
        ],
        name="own_slots",
    )(received)


def gelu(x):
    return 0.5 * x * (1.0 + jnp.tanh(math.sqrt(2.0 / math.pi) * (x + 0.044715 * (x * x * x))))


def expert_kernel(own, other, first, second, own_out, other_out):
    copies, rows, width = own.shape
    half = copies * rows
    both = jnp.concatenate([own[...].reshape(half, width), other[...].reshape(half, width)], axis=0)
    hidden = gelu(jnp.dot(both, first[0], preferred_element_type=F32)).astype(BF16)
    result = jnp.dot(hidden, second[0], preferred_element_type=F32)
    own_out[...] = result[:half].reshape(copies, rows, width)
    other_out[...] = result[half:].reshape(copies, rows, width).astype(BF16)


def expert_layers(own, other, w_in, w_out):
    copies, rows, width = own.shape
    experts, _, hidden = w_in.shape
    each = rows // experts
    rows_spec = pl.BlockSpec((copies, each, width), lambda e: (0, e, 0))
    return pl.pallas_call(
        expert_kernel,
        grid=(experts,),
        in_specs=[
            rows_spec,
            rows_spec,
            pl.BlockSpec((1, width, hidden), lambda e: (e, 0, 0)),
            pl.BlockSpec((1, hidden, width), lambda e: (e, 0, 0)),
        ],
        out_specs=[rows_spec, rows_spec],
        out_shape=[
            jax.ShapeDtypeStruct(own.shape, F32),
            jax.ShapeDtypeStruct(own.shape, BF16),
        ],
        name="experts",
    )(own, other, w_in, w_out)


def collect_kernel(seqs, experts, partial, result):
    total = jnp.sum(partial[...].astype(F32), axis=0).astype(BF16)
    per_expert = total.shape[0] // (seqs * experts)
    order = expert_order(seqs, experts, per_expert, True)
    ordered = jnp.dot(order, total, preferred_element_type=F32).astype(BF16)
    for s in range(result.shape[0]):
        result[s] = ordered


def collect(partial, seqs, experts, shards):
    _, rows, width = partial.shape
    return pl.pallas_call(
        functools.partial(collect_kernel, seqs, experts),
        out_shape=jax.ShapeDtypeStruct((shards, rows, width), BF16),
        name="collect",
    )(partial)


def combine_kernel(source, seq, mix, outputs, result):
    shards, owned, width = outputs.shape
    slots = outputs[...].reshape(shards * owned, width)
    result[0, 0] = jnp.dot(mix[0], slots, preferred_element_type=F32).astype(BF16)


def combine(source, seq, mixes, outputs, seqs):
    shards, block, slots = mixes.shape
    width = outputs.shape[2]
    owned = outputs.shape[1] // seqs
    blocks = source.shape[0]
    return pl.pallas_call(
        combine_kernel,
        grid_spec=pltpu.PrefetchScalarGridSpec(
            num_scalar_prefetch=2,
            grid=(blocks,),
            in_specs=[
                pl.BlockSpec((1, block, slots), lambda b, source, seq: (source[b], 0, 0)),
                pl.BlockSpec((shards, owned, width), lambda b, source, seq: (0, seq[b], 0)),
            ],
            out_specs=pl.BlockSpec((1, 1, block, width), lambda b, source, seq: (0, b, 0, 0)),
        ),
        out_shape=jax.ShapeDtypeStruct((1, blocks, block, width), BF16),
        name="combine",
    )(source, seq, mixes, outputs)


def swapped(array):
    return lax.ppermute(array, "c", [(0, 1), (1, 0)])


def exchanged(array, axis):
    return lax.all_to_all(array, axis, split_axis=0, concat_axis=0, tiled=True)


def local(tokens, slot_params, dest, lengths, w_in, w_out):
    seqs, length = tokens.shape[1:3]
    held = dest.shape[1] * dest.shape[2]
    shards = lax.axis_size(EXPERT)
    experts = w_in.shape[0]
    owned = slot_params.shape[1] // shards
    counts = lengths[0] - lax.axis_index(EXPERT) * length
    targets = dest.reshape(held)
    peers = targets // held
    block_seq = jnp.arange(held, dtype=jnp.int32) // dest.shape[2]
    code = targets % held * seqs + block_seq + 1
    to_shard = jnp.arange(shards, dtype=jnp.int32)
    labels = jnp.sum(jnp.where(peers[None, :] == to_shard[:, None], code[None, :], 0), axis=1)

    payload, mixes = dispatch(tokens, slot_params, counts, peers, labels, shards)
    received = exchanged(payload, EXPERT)
    slot_in, tags = own_slots(received, seqs, experts, lax.axis_size("y"), owned)
    mixes, slot_in = lax.optimization_barrier((mixes, slot_in))
    arrived = exchanged(mixes, EXPERT)

    own = exchanged(slot_in, "y")
    own_out, other_out = expert_layers(own, swapped(own), w_in, w_out)
    partial = (own_out + swapped(other_out).astype(F32)).astype(BF16)
    outputs = exchanged(collect(exchanged(partial, "y"), seqs, experts, shards), EXPERT)

    found = tags[:, LANES - 1].astype(jnp.int32) - 1
    place = jnp.where(found >= 0, found // seqs, -1)
    match = place[None, :] == jnp.arange(held, dtype=jnp.int32)[:, None]
    source = jnp.sum(jnp.where(match, to_shard[None, :], 0), axis=1)
    seq = jnp.sum(jnp.where(match, found[None, :] % seqs, 0), axis=1)
    return combine(source, seq, arrived, outputs, seqs)


def solution(mesh):
    finer = Mesh(mesh.devices.reshape(4, 2, 4, 4), DP + EXPERT)
    in_specs = (
        P(DP, None, EXPERT, None),
        P(),
        P(DP, None, EXPERT),
        P(DP, None),
        P(EXPERT, None, DP),
        P(EXPERT, DP, None),
    )
    out_specs = P(DP, EXPERT, None, None)
    return jax.shard_map(local, mesh=finer, in_specs=in_specs, out_specs=out_specs, check_vma=False)
```

time: 361 us -> 174 us (0.48)
  waiting for transfers between devices: 151 us -> 60.7 us
  blocking collectives: 104 us -> 63.1 us
  matrix products: 40.4 us -> 0 us
  local copies, waits for them, and re-layouts: 41.7 us -> 1.66 us
  Pallas kernels: 0 us -> 35.7 us
  starting transfers between devices: 15.3 us -> 8.29 us
    all_to_all x3 -> x2, waiting for transfers between devices: 151 us -> 56.8 us  [exchanged(): return lax.all_to_all(array, axis, split_axis=0, concat_axis=0, tiled=True)]
    dot_general x5 -> x0, matrix products: 40.4 us -> none  [the longest x1 12.1 us: local(): jnp.einsum('bq,bsd->qsd', member.astype(jnp.float32), block_numer, precis...]
    pallas_call x0 -> x5, Pallas kernels: none -> 35.7 us  [the longest x1 10.8 us: expert_layers(): pl.pallas_call(expert_kernel, grid=(experts,), in_specs=[rows_spec, rows_...]
    pmax x2 -> x0, blocking collectives: 22.4 us -> none  [over_axes(): array = lax.pmax(array, axis)]
    all_to_all x3, blocking collectives: 81.3 us -> 63.1 us  [exchanged(): return lax.all_to_all(array, axis, split_axis=0, concat_axis=0, tiled=True)]
    scatter x2 -> x0, local copies, waits for them, and re-layouts: 11.5 us -> none  [the longest x1 10.9 us: local(): jnp.zeros((shard_count, block_tokens, width), jnp.bfloat16).at[peer_device]]
    gather x2 -> x0, local copies, waits for them, and re-layouts: 10.6 us -> none  [the longest x1 6.21 us: local(): result = arrived[arrange(arrived_labels, held_blocks)]]
    all_to_all x3 -> x2, starting transfers between devices: 15.3 us -> 8.15 us  [exchanged(): return lax.all_to_all(array, axis, split_axis=0, concat_axis=0, tiled=True)]
  transfers between devices with their start and end apart: 3 -> 4, of which waited for: 2 -> 4; matrix products, arithmetic and copies ran while one was open for 9% -> 1% of each run, Pallas kernels for 0% -> 2%
where the time goes in v1:
time: 174 us
  blocking collectives  63.1 us (36%)
  waiting for transfers between devices  60.7 us (35%)
  Pallas kernels  35.7 us (21%)
  starting transfers between devices  8.29 us (5%)
  other arithmetic  4 us (2%)
    all_to_all x3, blocking collectives, exchanged(): return lax.all_to_all(array, axis, split_axis=0, concat_axis=0, tiled=True)  63.1 us
    all_to_all x2, waiting for transfers between devices, exchanged(): return lax.all_to_all(array, axis, split_axis=0, concat_axis=0, tiled=True)  56.8 us
    pallas_call x1, Pallas kernels, expert_layers(): pl.pallas_call(expert_kernel, grid=(experts,), in_specs=[rows_spec, rows_...  10.8 us
    pallas_call x1, Pallas kernels, dispatch(): pl.pallas_call(dispatch_kernel, grid_spec=pltpu.PrefetchScalarGridSpec(nu...  10.5 us
    pallas_call x1, Pallas kernels, combine(): pl.pallas_call(combine_kernel, grid_spec=pltpu.PrefetchScalarGridSpec(num...  8.34 us
    all_to_all x2, starting transfers between devices, exchanged(): return lax.all_to_all(array, axis, split_axis=0, concat_axis=0, tiled=True)  8.15 us
    ppermute x2, waiting for transfers between devices, swapped(): return lax.ppermute(array, 'c', [(0, 1), (1, 0)])  3.89 us
  transfers between devices with their start and end apart: 4, of which 4 were waited for; matrix products, arithmetic and copies ran while one was open for 1% of the time, Pallas kernels for 2%

profile of v1, /device:TPU:0, one launch (start us, length us, event | category | flops | bytes accessed | tf_op | source)
XLA Modules:
  0.0 173.5 jit_solution(3033381439239428510)
XLA Ops:
  0.0 0.8 copy.9
  0.8 0.1 reshape.116
  0.9 0.0 copy-start.4
  0.9 1.2 subtract_bitcast_fusion.counts
  2.0 0.6 select_reduce_fusion.2.labels
  2.6 0.0 copy-done.4
  2.6 10.5 %dispatch.1 = (bf16[16,528,128]{2,1,0:T(8,128)(2,1)}, bf16[16,256,256]{2,1,0:T(8,128)(2,1)}) custom-call(s32[4]{0:T(128)} %subtract_bitcast_fusion.counts, s32[8]{0:T(128)} %copy-done.4, s32[16]{0:T(128)} %select_reduce_fusion.2.labels, bf16[1,4,512,1024]{3,2,1,0:T(8,128)(2,1)} %tokens.1, bf16[1024,256]{1,0:T(8,128)(2,1)} %params.1), custom_call_target="tpu_custom_call" | custom-call | tf_op jit(solution)/shard_map/dispatch/pallas_call | solution.py:90
  13.1 37.2 %all_to_all.25.received = bf16[16,528,128]{2,1,0:T(8,128)(2,1)} all-to-all(bf16[16,528,128]{2,1,0:T(8,128)(2,1)} %get-tuple-element.13), channel_id=1, replica_groups=mesh['y'=4,'c'=2,'z'=4,'x'=4] {'z','x'}, dimensions={0} | all-to-all | bytes 4325376 | tf_op jit(solution)/shard_map/all_to_all | solution.py:251
  50.4 3.3 %own_slots.1 = (bf16[4,64,1024]{2,1,0:T(8,128)(2,1)}, f32[16,128]{1,0:T(8,128)}) custom-call(bf16[16,528,128]{2,1,0:T(8,128)(2,1)} %all_to_all.25.received), custom_call_target="tpu_custom_call" | custom-call | tf_op jit(solution)/shard_map/own_slots/pallas_call | solution.py:154
  53.7 12.7 %all_to_all.26.own = bf16[4,64,1024]{2,1,0:T(8,128)(2,1)S(1)} all-to-all(bf16[4,64,1024]{2,1,0:T(8,128)(2,1)} %get-tuple-element.18), channel_id=1, replica_groups=mesh['y'=4,'c'=2,'z'=4,'x'=4] {'y'}, dimensions={0} | all-to-all | bytes 1048576 | tf_op jit(solution)/shard_map/all_to_all | solution.py:251
  66.4 0.0 copy-start.1
  66.4 0.0 collective-permute-start
  66.4 1.9 %collective-permute-done.other = bf16[4,64,1024]{2,1,0:T(8,128)(2,1)S(1)} collective-permute-done((bf16[4,64,1024]{2,1,0:T(8,128)(2,1)S(1)}, bf16[4,64,1024]{2,1,0:T(8,128)(2,1)S(1)}, u32[]{:S(2)}, u32[]{:S(2)}) %collective-permute-start) | collective-permute-done | bytes 524320 | tf_op jit(solution)/shard_map/ppermute | solution.py:247
  68.3 0.0 copy-done.1
  68.3 0.0 copy-start.2
  68.3 0.8 copy-done.2
  69.1 10.8 %experts.1 = (f32[4,64,1024]{2,1,0:T(8,128)}, bf16[4,64,1024]{2,1,0:T(8,128)(2,1)}) custom-call(bf16[4,64,1024]{2,1,0:T(8,128)(2,1)} %copy-done.1, bf16[4,64,1024]{2,1,0:T(8,128)(2,1)} %copy-done.2, bf16[8,1024,512]{2,1,0:T(8,128)(2,1)} %first.1, bf16[8,512,1024]{2,1,0:T(8,128)(2,1)} %second.1), custom_call_target="tpu_custom_call" | custom-call | tf_op jit(solution)/shard_map/experts/pallas_call | solution.py:183
  79.9 0.1 collective-permute-start.1
  80.1 2.0 %collective-permute-done.1 = bf16[4,64,1024]{2,1,0:T(8,128)(2,1)S(1)} collective-permute-done((bf16[4,64,1024]{2,1,0:T(8,128)(2,1)}, bf16[4,64,1024]{2,1,0:T(8,128)(2,1)S(1)}, u32[]{:S(2)}, u32[]{:S(2)}) %collective-permute-start.1) | collective-permute-done | bytes 524320 | tf_op jit(solution)/shard_map/ppermute | solution.py:247
  82.0 1.4 add_convert_fusion
  83.4 13.1 %all_to_all.27.partial = bf16[4,64,1024]{2,1,0:T(8,128)(2,1)} all-to-all(bf16[4,64,1024]{2,1,0:T(8,128)(2,1)S(1)} %add_convert_fusion), channel_id=1, replica_groups=mesh['y'=4,'c'=2,'z'=4,'x'=4] {'y'}, dimensions={0} | all-to-all | bytes 1048576 | tf_op jit(solution)/shard_map/all_to_all | solution.py:251
  96.6 3.7 %all-to-all-start.1 = ((bf16[16,256,256]{2,1,0:T(8,128)(2,1)}), bf16[16,256,256]{2,1,0:T(8,128)(2,1)S(1)}, u32[]{:S(2)}, u32[]{:S(2)}) async-start(bf16[16,256,256]{2,1,0:T(8,128)(2,1)} %get-tuple-element.17), calls=%async_computation.1 | async-start | bytes 4194304 | tf_op jit(solution)/shard_map/all_to_all | solution.py:251
  100.3 2.7 %collect.1 = bf16[16,64,1024]{2,1,0:T(8,128)(2,1)} custom-call(bf16[4,64,1024]{2,1,0:T(8,128)(2,1)} %all_to_all.27.partial), custom_call_target="tpu_custom_call" | custom-call | tf_op jit(solution)/shard_map/collect/pallas_call | solution.py:212
  103.0 0.0 copy-start.3
  103.0 28.3 %all-to-all-done.1.mix = bf16[16,256,256]{2,1,0:T(8,128)(2,1)S(1)} async-done(((bf16[16,256,256]{2,1,0:T(8,128)(2,1)}), bf16[16,256,256]{2,1,0:T(8,128)(2,1)S(1)}, u32[]{:S(2)}, u32[]{:S(2)}) %all-to-all-start.1) | async-done | bytes 2097184 | tf_op jit(solution)/shard_map/all_to_all | solution.py:251
  131.3 0.0 copy-start
  131.3 4.4 %all-to-all-start.4 = ((bf16[16,64,1024]{2,1,0:T(8,128)(2,1)}), bf16[16,64,1024]{2,1,0:T(8,128)(2,1)}, u32[]{:S(2)}, u32[]{:S(2)}) async-start(bf16[16,64,1024]{2,1,0:T(8,128)(2,1)} %collect.1), calls=%async_computation.4 | async-start | bytes 4194304 | tf_op jit(solution)/shard_map/all_to_all | solution.py:251
  135.7 0.0 copy-done.3
  135.8 0.2 add_reduce_fusion
  136.0 0.7 select_reduce_fusion
  136.6 28.5 %all-to-all-done.4.outputs = bf16[16,64,1024]{2,1,0:T(8,128)(2,1)} async-done(((bf16[16,64,1024]{2,1,0:T(8,128)(2,1)}), bf16[16,64,1024]{2,1,0:T(8,128)(2,1)}, u32[]{:S(2)}, u32[]{:S(2)}) %all-to-all-start.4) | async-done | bytes 2097184 | tf_op jit(solution)/shard_map/all_to_all | solution.py:251
  165.2 0.0 copy-done
  165.2 8.3 %combine.1 = bf16[1,8,256,1024]{3,2,1,0:T(8,128)(2,1)} custom-call(s32[8]{0:T(128)} %get-tuple-element.22.source, s32[8]{0:T(128)} %get-tuple-element.21.seq, bf16[16,256,256]{2,1,0:T(8,128)(2,1)} %copy-done, bf16[16,64,1024]{2,1,0:T(8,128)(2,1)} %all-to-all-done.4.outputs), custom_call_target="tpu_custom_call" | custom-call | tf_op jit(solution)/shard_map/combine/pallas_call | solution.py:230
  (2 shorter events, 0.0 us)
Async XLA Ops:
  0.9 1.8 %copy-start.4 = (s32[8]{0:T(128)}, s32[8]{0:T(128)S(1)}, u32[]{:S(2)}) copy-start(s32[8]{0:T(128)S(1)} %get-tuple-element.26.peers) | copy-start | bytes 100
  66.4 1.9 %copy-start.1 = (bf16[4,64,1024]{2,1,0:T(8,128)(2,1)}, bf16[4,64,1024]{2,1,0:T(8,128)(2,1)S(1)}, u32[]{:S(2)}) copy-start(bf16[4,64,1024]{2,1,0:T(8,128)(2,1)S(1)} %all_to_all.26.own) | copy-start | bytes 1572868
  66.4 1.9 %collective-permute-start = (bf16[4,64,1024]{2,1,0:T(8,128)(2,1)S(1)}, bf16[4,64,1024]{2,1,0:T(8,128)(2,1)S(1)}, u32[]{:S(2)}, u32[]{:S(2)}) collective-permute-start(bf16[4,64,1024]{2,1,0:T(8,128)(2,1)S(1)} %all_to_all.26.own), channel_id=1, source_target_pairs={{0,16},{16,0},{1,17},{17,1},{2,18},{18,2},{3,19},{19,3},{4,20},{20... | collective-permute-start | bytes 1572872 | tf_op jit(solution)/shard_map/ppermute | solution.py:247
  68.3 0.8 copy-start.2
  79.9 2.1 %collective-permute-start.1 = (bf16[4,64,1024]{2,1,0:T(8,128)(2,1)}, bf16[4,64,1024]{2,1,0:T(8,128)(2,1)S(1)}, u32[]{:S(2)}, u32[]{:S(2)}) collective-permute-start(bf16[4,64,1024]{2,1,0:T(8,128)(2,1)} %get-tuple-element.20), channel_id=1, source_target_pairs={{0,16},{16,0},{1,17},{17,1},{2,18},{18,2},{3,19},{19,3},{4,20},{20... | collective-permute-start | bytes 1572872 | tf_op jit(solution)/shard_map/ppermute | solution.py:247
  96.6 34.7 %all-to-all-start.1 = ((bf16[16,256,256]{2,1,0:T(8,128)(2,1)}), bf16[16,256,256]{2,1,0:T(8,128)(2,1)S(1)}, u32[]{:S(2)}, u32[]{:S(2)}) async-start(bf16[16,256,256]{2,1,0:T(8,128)(2,1)} %get-tuple-element.17), calls=%async_computation.1 | async-start | bytes 4194304 | tf_op jit(solution)/shard_map/all_to_all | solution.py:251
  103.0 32.7 %copy-start.3 = (f32[16,128]{1,0:T(8,128)S(1)}, f32[16,128]{1,0:T(8,128)}, u32[]{:S(2)}) copy-start(f32[16,128]{1,0:T(8,128)} %get-tuple-element.14) | copy-start | bytes 24580
  131.3 33.9 %copy-start = (bf16[16,256,256]{2,1,0:T(8,128)(2,1)}, bf16[16,256,256]{2,1,0:T(8,128)(2,1)S(1)}, u32[]{:S(2)}) copy-start(bf16[16,256,256]{2,1,0:T(8,128)(2,1)S(1)} %all-to-all-done.1.mix) | copy-start | bytes 6291460
  131.3 33.9 %all-to-all-start.4 = ((bf16[16,64,1024]{2,1,0:T(8,128)(2,1)}), bf16[16,64,1024]{2,1,0:T(8,128)(2,1)}, u32[]{:S(2)}, u32[]{:S(2)}) async-start(bf16[16,64,1024]{2,1,0:T(8,128)(2,1)} %collect.1), calls=%async_computation.4 | async-start | bytes 4194304 | tf_op jit(solution)/shard_map/all_to_all | solution.py:251
